TPU v7x, 32 devices: a whole 2x2x4 slice. The times are simulated.
32 devices in a mesh: pts: 8 (over z, core), head: 4 (over y, x).
Axes of the slice: x: 2, y: 2, z: 4, core: 2. Of those that a mesh axis runs over, the one named last changes fastest.
Arguments:
- points: bfloat16 [73728, 128], P('pts')
- counts: int32 [8], P('pts'), may hold values from 1 to 9216, 55296 in all
- ln1_gain: float32 [2, 128], replicated, may hold values from 0.5 to 1.5
- ln1_bias: float32 [2, 128], replicated, may hold values from -1.5 to 1.5
- w_in: bfloat16 [2, 128, 128], P(None, None, 'head'), may hold values from -0.5 to 0.5
- w_fx: bfloat16 [2, 128, 128], P(None, None, 'head'), may hold values from -0.5 to 0.5
- w_slice: bfloat16 [2, 32, 32], replicated
- temper: float32 [2, 4], replicated, may hold values from 0.5 to 2
- query_weight: bfloat16 [2, 32, 32], replicated
- key_weight: bfloat16 [2, 32, 32], replicated, may hold values from -1 to 1
- value_weight: bfloat16 [2, 32, 32], replicated, may hold values from -1 to 1
- w_out: bfloat16 [2, 128, 128], P(None, 'head'), may hold values from -1 to 1
- b_out: float32 [2, 128], replicated, may hold values from -1.5 to 1.5
- ln2_gain: float32 [2, 128], replicated, may hold values from 0.5 to 1.5
- ln2_bias: float32 [2, 128], replicated, may hold values from -1.5 to 1.5
- w_up: bfloat16 [2, 128, 512], replicated, may hold values from -0.5 to 0.5
- w_down: bfloat16 [2, 512, 128], replicated, may hold values from -0.25 to 0.25
Outputs:
- features: bfloat16 [73728, 128], P(('pts', 'head'))
Inputs may be any that keep to these rules, and one draw needn't show every extreme that they name: counts[i] live points fill the first slots of shard i; at least one shard is full; they sum to 55296.
All inputs are finite; a program needn't handle non-finite values.
Results may differ from a plain program's by a relative error of at most 0.014.
Values may be sent and summed in bfloat16 or wider, within the bound.
A program may use at most 128 MiB of HBM per device.

v0:
```python
import jax
import jax.numpy as jnp
from jax import lax
from jax.sharding import PartitionSpec as P

DH = 32
M = 32


def layer_norm(value, gain, bias):
    mean = jnp.mean(value, axis=-1, keepdims=True)
    centred = value - mean
    var = jnp.mean(centred * centred, axis=-1, keepdims=True)
    return centred * lax.rsqrt(var + 1e-05) * gain + bias


def slice_attention(token_rows, query_weight, key_weight, value_weight):
    head_parts = lax.Precision.HIGHEST
    query_rows = jnp.einsum(
        "aur,rz->auz", token_rows, query_weight.astype(jnp.float32), precision=head_parts
    )
    slice_keys = jnp.einsum(
        "aur,rz->auz", token_rows, key_weight.astype(jnp.float32), precision=head_parts
    )
    slice_values = jnp.einsum(
        "aur,rz->auz", token_rows, value_weight.astype(jnp.float32), precision=head_parts
    )
    scores = jnp.einsum("hme,hke->hmk", query_rows, slice_keys, precision=head_parts) * DH ** (-0.5)
    attn = jax.nn.softmax(scores, axis=-1)
    return jnp.einsum("hmk,hke->hme", attn, slice_values, precision=head_parts).astype(jnp.bfloat16)


def body(
    points,
    counts,
    ln1_gain,
    ln1_bias,
    w_in,
    w_fx,
    w_slice,
    temper,
    query_weight,
    key_weight,
    value_weight,
    w_out,
    b_out,
    ln2_gain,
    ln2_bias,
    w_up,
    w_down,
):
    groups = lax.axis_size("head")
    rows = points.shape[0] // groups
    first_row = lax.axis_index("head") * rows
    layers = w_in.shape[0]
    full_in = lax.all_gather(w_in, "head", axis=2, tiled=True)
    full_fx = lax.all_gather(w_fx, "head", axis=2, tiled=True)
    full_out = lax.all_gather(w_out, "head", axis=1, tiled=True)
    heads = full_in.shape[2] // DH
    live = (first_row + jnp.arange(rows, dtype=jnp.int32) < counts[0]).astype(jnp.float32)
    current = lax.dynamic_slice_in_dim(points, first_row, rows, 0)
    for layer_index in range(layers):
        normed = layer_norm(
            current.astype(jnp.float32), ln1_gain[layer_index], ln1_bias[layer_index]
        ).astype(jnp.bfloat16)
        mid = jnp.dot(normed, full_in[layer_index], preferred_element_type=jnp.float32).astype(
            jnp.bfloat16
        )
        feats = jnp.dot(normed, full_fx[layer_index], preferred_element_type=jnp.float32).astype(
            jnp.bfloat16
        )
        spread = jnp.kron(jnp.eye(heads, dtype=jnp.bfloat16), w_slice[layer_index])
        logits = jnp.dot(mid, spread, preferred_element_type=jnp.float32)
        logits = logits.reshape(rows, heads, M) / temper[layer_index][None, :, None]
        weights = jax.nn.softmax(logits, axis=-1) * live[:, None, None]
        half_weights = weights.astype(jnp.bfloat16).reshape(rows, heads * M)
        total = jnp.sum(weights, axis=0)
        square = jnp.einsum("rs,rl->sl", half_weights, feats, preferred_element_type=jnp.float32)
        square = square.reshape(heads, M, heads, DH)
        numerator = jnp.stack([square[h, :, h, :] for h in range(heads)])
        numerator, total = lax.psum((numerator, total), ("pts", "head"))
        token_rows = numerator / jnp.maximum(total, 1.0)[..., None]
        mixed_token = slice_attention(
            token_rows,
            query_weight[layer_index],
            key_weight[layer_index],
            value_weight[layer_index],
        )
        wide = (
            jnp.einsum(
                "hmv,hvc->hmc",
                mixed_token,
                full_out[layer_index].reshape(heads, DH, -1),
                preferred_element_type=jnp.float32,
            )
            .astype(jnp.bfloat16)
            .reshape(heads * M, -1)
        )
        projected = jnp.dot(half_weights, wide, preferred_element_type=jnp.float32)
        after = current.astype(jnp.float32) + projected + b_out[layer_index]
        normed2 = layer_norm(after, ln2_gain[layer_index], ln2_bias[layer_index]).astype(
            jnp.bfloat16
        )
        upper = jax.nn.gelu(
            jnp.dot(normed2, w_up[layer_index], preferred_element_type=jnp.float32)
        ).astype(jnp.bfloat16)
        current = (
            after + jnp.dot(upper, w_down[layer_index], preferred_element_type=jnp.float32)
        ).astype(jnp.bfloat16)
    return current


def solution(mesh):
    placed = (
        P("pts", None),
        P("pts"),
        P(),
        P(),
        P(None, None, "head"),
        P(None, None, "head"),
        P(),
        P(),
        P(),
        P(),
        P(),
        P(None, "head", None),
        P(),
        P(),
        P(),
        P(),
        P(),
    )
    return jax.shard_map(
        body, mesh=mesh, in_specs=placed, out_specs=P(("pts", "head"), None), check_vma=False
    )
```

profile of v0, /device:TPU:0, one launch (start us, length us, event | category | flops | bytes accessed | tf_op | source)
XLA Modules:
  0.0 157.5 jit_solution(5383199505180625222)
XLA Ops:
  0.0 1.7 %copy-done = bf16[9216,128]{1,0:T(8,128)(2,1)S(1)} copy-done((bf16[9216,128]{1,0:T(8,128)(2,1)S(1)}, bf16[9216,128]{1,0:T(8,128)(2,1)}, u32[]{:S(2)}) %copy-start) | copy-done | bytes 2359320
  1.7 0.0 copy-start.13
  1.7 0.2 copy.26
  2.0 0.0 copy-start.18
  2.0 0.0 copy-start.19
  2.0 0.0 copy-start.10
  2.0 0.0 copy-start.16
  2.0 0.1 convert_reduce_fusion
  2.1 0.2 fusion.33
  2.3 0.3 copy-done.18
  2.7 0.0 copy-done.19
  2.7 0.6 slice_bitcast_fusion.34
  3.3 0.1 copy.19
  3.4 0.1 copy.20
  3.5 0.8 broadcast_multiply_fusion
  4.3 0.1 mul.187
  4.4 9.7 %all_gather.9 = bf16[2,128,128]{1,2,0:T(8,128)(2,1)S(1)} all-gather(bf16[2,128,32]{1,2,0:T(8,128)(2,1)S(1)} %copy-done.10), channel_id=1, replica_groups=mesh['pts'=8,'head'=4] {'head'}, dimensions={2}, use_global_device_ids=true | all-gather | bytes 81920 | tf_op jit(solution)/shard_map/all_gather | solution.py:56
  14.2 1.9 %fusion.122 = (f32[2304,4]{0,1:T(4,128)S(1)}, f32[2304,4,32]{0,2,1:T(8,128)}) fusion(bf16[4,32,128]{2,1,0:T(8,128)(2,1)S(1)} %bitcast.209, f32[4]{0:T(128)S(1)} %get-tuple-element.28, bf16[2,128,128]{1,2,0:T(8,128)(2,1)S(1)} %all_gather.9, bf16[2304,128]{0,1:T(8,128)(2,1)S(1)} %copy.26, f32[128]{0:T(128)S(1)} %get-tuple-element.34, ...), kind=kOutput, calls=%fused_computation.175 | convolution fusion | flops 153944096 | bytes 1897984 | tf_op jit(solution)/shard_map/sub | solution.py:75
  16.0 0.0 copy-start.11
  16.7 1.6 %fusion.57 = f32[4,32]{1,0:T(4,128)S(1)} fusion(f32[2304]{0:T(1024)S(1)} %fusion.83, f32[2304,4,32]{0,2,1:T(8,128)} %get-tuple-element.36, f32[2304,4]{0,1:T(4,128)S(1)} %get-tuple-element.35), kind=kLoop, calls=%fused_computation.77 | loop fusion | flops 884608 | bytes 1226240 | tf_op jit(solution)/shard_map/reduce_sum | solution.py:77
  18.3 8.2 %all_gather.10 = bf16[2,128,128]{1,2,0:T(8,128)(2,1)S(1)} all-gather(bf16[2,128,32]{1,2,0:T(8,128)(2,1)S(1)} %copy-done.11), channel_id=1, replica_groups=mesh['pts'=8,'head'=4] {'head'}, dimensions={2}, use_global_device_ids=true | all-gather | bytes 81920 | tf_op jit(solution)/shard_map/all_gather | solution.py:57
  26.5 0.4 convolution_convert_fusion.1
  27.0 0.0 copy-start.23
  27.0 0.0 copy-start.24
  27.0 0.0 copy-start.25
  27.0 0.6 fusion.39
  27.6 0.0 copy-start.12
  27.6 0.0 copy-start.17
  27.7 40.2 %all-reduce.1 = (f32[4,32,32]{2,1,0:T(8,128)S(1)}, f32[4,32]{1,0:T(4,128)S(1)}) all-reduce(f32[4,32,32]{2,1,0:T(8,128)S(1)} %pad_maximum_fusion, f32[4,32]{1,0:T(4,128)S(1)} %fusion.57), channel_id=1, replica_groups=mesh['pts'=8,'head'=4] {'pts','head'}, use_global_device_ids=true, to_apply=%region_4.5 | all-reduce | flops 4224 | bytes 33792 | tf_op jit(solution)/shard_map/psum | solution.py:81
  67.9 0.2 fusion.92
  68.2 0.2 fusion.94
  68.4 0.2 fusion.125
  68.7 0.2 fusion.90
  69.0 0.3 convolution_convert_fusion.7
  69.3 9.0 %all_gather.11 = bf16[2,128,128]{2,1,0:T(8,128)(2,1)S(1)} all-gather(bf16[2,32,128]{2,1,0:T(8,128)(2,1)S(1)} %copy-done.12), channel_id=1, replica_groups=mesh['pts'=8,'head'=4] {'head'}, dimensions={1}, use_global_device_ids=true | all-gather | bytes 81920 | tf_op jit(solution)/shard_map/all_gather | solution.py:58
  78.3 0.6 fusion.121
  78.9 0.5 slice_bitcast_fusion.32
  79.4 2.8 %fusion.126 = (f32[2304]{0:T(1024)S(1)}, f32[2304,128]{0,1:T(8,128)}) fusion(f32[128]{0:T(128)S(1)} %get-tuple-element.26, bf16[4,32,32]{2,1,0:T(8,128)(2,1)S(1)} %convolution_convert_fusion.7, bf16[4,32,128]{2,1,0:T(8,128)(2,1)S(1)} %bitcast.212, f32[2304]{0:T(1024)S(1)} %fusion.83, f32[2304,4,32]{0,2,1:T(8,128)} %get-tuple-element.36, ...), kind=kOutput, calls=%fused_computation.177 | convolution fusion | flops 78624512 | bytes 3045888 | tf_op jit(solution)/shard_map/dot_general | solution.py:99
  82.2 1.4 multiply_reduce_fusion.2
  83.6 0.6 add_rsqrt_fusion.2
  84.2 0.6 slice_bitcast_fusion.30
  84.8 4.6 %fusion.127 = (f32[2304]{0:T(1024)}, f32[2304,128]{0,1:T(8,128)S(1)}) fusion(f32[2304,128]{0,1:T(8,128)} %get-tuple-element.40, bf16[2,512,128]{2,1,0:T(8,128)(2,1)} %param.33, f32[128]{0:T(128)} %get-tuple-element.24, f32[128]{0:T(128)} %get-tuple-element.51, f32[2304]{0:T(1024)} %add_rsqrt_fusion.2, f32[2304]{0:T(1024)} %copy-done.8, ...), kind=kOutput, calls=%fused_computation.178 | convolution fusion | flops 617248512 | bytes 3835904 | tf_op jit(solution)/shard_map/dot_general | solution.py:108
  89.4 0.7 broadcast_multiply_fusion.3
  90.1 0.1 multiply_reduce_fusion.1
  90.3 1.2 add_convert_fusion.1
  91.5 1.6 %mul.210 = bf16[128,128]{0,1:T(8,128)(2,1)} reshape(bf16[4,32,4,32]{1,0,3,2:T(4,128)(2,1)} %get-tuple-element.29) | data formatting | bytes 65536 | tf_op jit(solution)/shard_map/jit(kron)/mul | solution.py:72
  93.1 3.4 %fusion.130 = (f32[2304,4]{0,1:T(4,128)}, f32[2304,4,32]{0,2,1:T(8,128)}) fusion(bf16[4,32,128]{2,1,0:T(8,128)(2,1)} %bitcast.210, bf16[2304,128]{0,1:T(8,128)(2,1)} %add_convert_fusion.1, f32[4]{0:T(128)S(1)} %get-tuple-element.27, bf16[2,128,128]{1,2,0:T(8,128)(2,1)} %copy-done.7), kind=kOutput, calls=%fused_computation.179 | convolution fusion | flops 152174624 | bytes 1871888 | tf_op jit(solution)/shard_map/sub | solution.py:75
  96.5 1.6 %fusion.59 = f32[4,32]{1,0:T(4,128)S(1)} fusion(f32[2304]{0:T(1024)S(1)} %fusion.83, f32[2304,4,32]{0,2,1:T(8,128)} %get-tuple-element.44, f32[2304,4]{0,1:T(4,128)} %get-tuple-element.43), kind=kLoop, calls=%fused_computation.79 | loop fusion | flops 884608 | bytes 1226240 | tf_op jit(solution)/shard_map/reduce_sum | solution.py:77
  98.2 0.3 convolution_convert_fusion
  98.5 0.6 fusion.37
  99.1 0.6 pad_maximum_fusion.1
  99.7 40.3 %all-reduce = (f32[4,32,32]{2,1,0:T(8,128)}, f32[4,32]{1,0:T(4,128)}) all-reduce(f32[4,32,32]{2,1,0:T(8,128)} %pad_maximum_fusion.1, f32[4,32]{1,0:T(4,128)S(1)} %fusion.59), channel_id=1, replica_groups=mesh['pts'=8,'head'=4] {'pts','head'}, use_global_device_ids=true, to_apply=%region_15.16 | all-reduce | flops 4224 | bytes 33792 | tf_op jit(solution)/shard_map/psum | solution.py:81
  140.0 0.7 broadcast_maximum_fusion
  140.7 1.1 fusion.86
  141.8 1.1 fusion.88
  142.9 0.2 fusion.131
  143.1 1.1 fusion.84
  144.2 0.9 convolution_convert_fusion.5
  145.2 3.4 %fusion.132 = (f32[2304]{0:T(1024)}, f32[2304,128]{0,1:T(8,128)}) fusion(f32[128]{0:T(128)} %get-tuple-element.25, f32[2304,128]{0,1:T(8,128)S(1)} %get-tuple-element.42, bf16[4,32,32]{2,1,0:T(8,128)(2,1)} %convolution_convert_fusion.5, bf16[4,32,128]{2,1,0:T(8,128)(2,1)} %bitcast.211, f32[2304]{0:T(1024)S(1)} %fusion.83, ...), kind=kOutput, calls=%fused_computation.181 | convolution fusion | flops 78329600 | bytes 3635712 | tf_op jit(solution)/shard_map/dot_general | solution.py:99
  148.6 0.8 broadcast_multiply_fusion.2
  149.4 1.4 multiply_reduce_fusion
  150.8 0.6 add_rsqrt_fusion
  151.4 4.0 %fusion.27 = bf16[2304,128]{0,1:T(8,128)(2,1)} fusion(f32[2304,128]{0,1:T(8,128)S(1)} %copy-done.4, f32[128]{0:T(128)S(1)} %copy-done.22, f32[128]{0:T(128)} %get-tuple-element.52, f32[2304]{0:T(1024)} %add_rsqrt_fusion, f32[2304]{0:T(1024)S(1)} %broadcast_multiply_fusion.2, bf16[2,512,128]{2,1,0:T(8,128)(2,1)} %param.33, bf16[2,128,512]{2,1,0:T(8,128)(2,1)} %param.32), kind=kOutput, calls=%fused_computation.35 | convolution fusion | flops 616660992 | bytes 3236864 | tf_op jit(solution)/shard_map/dot_general | solution.py:108
  155.4 2.1 %copy.22 = bf16[2304,128]{1,0:T(8,128)(2,1)} copy(bf16[2304,128]{0,1:T(8,128)(2,1)} %fusion.27) | data formatting | bytes 1179648 | tf_op jit(solution)/shard_map/convert_element_type | solution.py:109
  (53 shorter events, 0.3 us)
Async XLA Ops:
  0.0 1.7 %copy-start = (bf16[9216,128]{1,0:T(8,128)(2,1)S(1)}, bf16[9216,128]{1,0:T(8,128)(2,1)}, u32[]{:S(2)}) copy-start(bf16[9216,128]{1,0:T(8,128)(2,1)} %param.17) | copy-start | bytes 7077892
  1.7 1.6 copy-start.13
  2.0 0.7 copy-start.18
  2.0 0.7 copy-start.19
  2.0 2.4 %copy-start.10 = (bf16[2,128,32]{1,2,0:T(8,128)(2,1)S(1)}, bf16[2,128,32]{1,2,0:T(8,128)(2,1)}, u32[]{:S(2)}) copy-start(bf16[2,128,32]{1,2,0:T(8,128)(2,1)} %param.21) | copy-start | bytes 49156
  2.0 12.1 %copy-start.16 = (f32[2,4]{1,0:T(2,128)S(1)}, f32[2,4]{1,0:T(2,128)}, u32[]{:S(2)}) copy-start(f32[2,4]{1,0:T(2,128)} %param.24) | copy-start | bytes 100
  14.1 1.9 %copy-start.7 = (bf16[2,128,128]{1,2,0:T(8,128)(2,1)}, bf16[2,128,128]{1,2,0:T(8,128)(2,1)S(1)}, u32[]{:S(2)}) copy-start(bf16[2,128,128]{1,2,0:T(8,128)(2,1)S(1)} %all_gather.9) | copy-start | bytes 196612
  16.0 2.3 %copy-start.11 = (bf16[2,128,32]{1,2,0:T(8,128)(2,1)S(1)}, bf16[2,128,32]{1,2,0:T(8,128)(2,1)}, u32[]{:S(2)}) copy-start(bf16[2,128,32]{1,2,0:T(8,128)(2,1)} %param.22) | copy-start | bytes 49156
  16.7 10.3 %copy-start.2 = (f32[2304,4,32]{0,2,1:T(8,128)S(1)}, f32[2304,4,32]{0,2,1:T(8,128)}, u32[]{:S(2)}) copy-start(f32[2304,4,32]{0,2,1:T(8,128)} %get-tuple-element.36) | copy-start | bytes 3538948
  26.5 1.1 copy-start.5
  27.0 40.9 %copy-start.23 = (bf16[2,32,32]{2,1,0:T(8,128)(2,1)S(1)}, bf16[2,32,32]{2,1,0:T(8,128)(2,1)}, u32[]{:S(2)}) copy-start(bf16[2,32,32]{2,1,0:T(8,128)(2,1)} %param.26) | copy-start | bytes 12292
  27.0 41.2 %copy-start.24 = (bf16[2,32,32]{2,1,0:T(8,128)(2,1)S(1)}, bf16[2,32,32]{2,1,0:T(8,128)(2,1)}, u32[]{:S(2)}) copy-start(bf16[2,32,32]{2,1,0:T(8,128)(2,1)} %param.25) | copy-start | bytes 12292
  27.0 41.7 %copy-start.25 = (bf16[2,32,32]{2,1,0:T(8,128)(2,1)S(1)}, bf16[2,32,32]{2,1,0:T(8,128)(2,1)}, u32[]{:S(2)}) copy-start(bf16[2,32,32]{2,1,0:T(8,128)(2,1)} %param.27) | copy-start | bytes 12292
  27.6 41.6 %copy-start.12 = (bf16[2,32,128]{2,1,0:T(8,128)(2,1)S(1)}, bf16[2,32,128]{2,1,0:T(8,128)(2,1)}, u32[]{:S(2)}) copy-start(bf16[2,32,128]{2,1,0:T(8,128)(2,1)} %param.28) | copy-start | bytes 49156
  27.6 51.2 %copy-start.17 = (f32[2,128]{1,0:T(2,128)S(1)}, f32[2,128]{1,0:T(2,128)}, u32[]{:S(2)}) copy-start(f32[2,128]{1,0:T(2,128)} %param.29) | copy-start | bytes 3076
  82.2 2.1 %copy-start.20 = (f32[2,128]{1,0:T(2,128)S(1)}, f32[2,128]{1,0:T(2,128)}, u32[]{:S(2)}) copy-start(f32[2,128]{1,0:T(2,128)} %param.31) | copy-start | bytes 3076
  82.2 2.1 %copy-start.21 = (f32[2,128]{1,0:T(2,128)S(1)}, f32[2,128]{1,0:T(2,128)}, u32[]{:S(2)}) copy-start(f32[2,128]{1,0:T(2,128)} %param.30) | copy-start | bytes 3076
  82.2 2.7 %copy-start.8 = (f32[2304]{0:T(1024)}, f32[2304]{0:T(1024)S(1)}, u32[]{:S(2)}) copy-start(f32[2304]{0:T(1024)S(1)} %broadcast_multiply_fusion.4) | copy-start | bytes 27652
  89.4 0.9 copy-start.14
  89.4 0.9 copy-start.15
  96.5 1.6 %copy-start.1 = (bf16[2304,128]{0,1:T(8,128)(2,1)S(1)}, bf16[2304,128]{0,1:T(8,128)(2,1)}, u32[]{:S(2)}) copy-start(bf16[2304,128]{0,1:T(8,128)(2,1)} %add_convert_fusion.1) | copy-start | bytes 1769476
  96.5 1.6 %copy-start.6 = (bf16[2,128,128]{1,2,0:T(8,128)(2,1)S(1)}, bf16[2,128,128]{1,2,0:T(8,128)(2,1)}, u32[]{:S(2)}) copy-start(bf16[2,128,128]{1,2,0:T(8,128)(2,1)} %copy-done.5) | copy-start | bytes 196612
  96.5 2.0 %copy-start.3 = (f32[2304,4,32]{0,2,1:T(8,128)S(1)}, f32[2304,4,32]{0,2,1:T(8,128)}, u32[]{:S(2)}) copy-start(f32[2304,4,32]{0,2,1:T(8,128)} %get-tuple-element.44) | copy-start | bytes 3538948
  96.5 2.0 %copy-start.9 = (f32[2304,4]{0,1:T(4,128)S(1)}, f32[2304,4]{0,1:T(4,128)}, u32[]{:S(2)}) copy-start(f32[2304,4]{0,1:T(4,128)} %get-tuple-element.43) | copy-start | bytes 110596
  148.6 2.8 %copy-start.4 = (f32[2304,128]{0,1:T(8,128)S(1)}, f32[2304,128]{0,1:T(8,128)}, u32[]{:S(2)}) copy-start(f32[2304,128]{0,1:T(8,128)} %get-tuple-element.48) | copy-start | bytes 3538948
  148.6 2.8 %copy-start.22 = (f32[128]{0:T(128)S(1)}, f32[128]{0:T(128)}, u32[]{:S(2)}) copy-start(f32[128]{0:T(128)} %get-tuple-element.23) | copy-start | bytes 1540
where the time goes:
time: 159 us; the launch traced here: 158 us
  blocking collectives  107 us (67%)
  matrix products  27.6 us (17%)
  other arithmetic  12.6 us (8%)
  local copies, waits for them, and re-layouts  8.79 us (6%)
    psum x2, blocking collectives, body(): numerator, total = lax.psum((numerator, total), ('pts', 'head'))  80.5 us
    all_gather x1, blocking collectives, body(): full_in = lax.all_gather(w_in, 'head', axis=2, tiled=True)  9.72 us
    all_gather x1, blocking collectives, body(): full_out = lax.all_gather(w_out, 'head', axis=1, tiled=True)  9 us
    dot_general x2, matrix products, body(): jnp.dot(upper, w_down[layer_index], preferred_element_type=jnp.float32)  8.51 us
    all_gather x1, blocking collectives, body(): full_fx = lax.all_gather(w_fx, 'head', axis=2, tiled=True)  8.21 us
    dot_general x2, matrix products, body(): projected = jnp.dot(half_weights, wide, preferred_element_type=jnp.float32)  6.22 us
    sub x2, matrix products, body(): weights = jax.nn.softmax(logits, axis=-1) * live[:, None, None]  5.29 us
    reduce_sum x2, other arithmetic, body(): total = jnp.sum(weights, axis=0)  3.22 us

commit v1 on v0

--- a/solution.py
+++ b/solution.py
@@ -53,7 +53,7 @@
     rows = points.shape[0] // groups
     first_row = lax.axis_index("head") * rows
     layers = w_in.shape[0]
-    full_in = lax.all_gather(w_in, "head", axis=2, tiled=True)
+    full_in = jnp.concatenate(lax.all_gather(w_in, "head"), axis=2)
     full_fx = lax.all_gather(w_fx, "head", axis=2, tiled=True)
     full_out = lax.all_gather(w_out, "head", axis=1, tiled=True)
     heads = full_in.shape[2] // DH

time: 159 us -> 164 us (1.031)
  matrix products: 27.6 us -> 32.3 us
  other arithmetic: 12.6 us -> 8.35 us
  local copies, waits for them, and re-layouts: 8.79 us -> 12.7 us
    dot_general x2, matrix products: 1.2 us -> 4.24 us  [body(): jnp.einsum('rs,rl->sl', half_weights, feats, preferred_element_type=jnp.f...]
    all_gather x1, blocking collectives: 8.21 us -> 11.1 us  [body(): full_fx = lax.all_gather(w_fx, 'head', axis=2, tiled=True)]
    reduce_sum x2, other arithmetic: 3.22 us -> 0.44 us  [body(): total = jnp.sum(weights, axis=0)]
    all_gather x1, blocking collectives: 9.72 us -> 7.44 us  [body(): full_in = jnp.concatenate(lax.all_gather(w_in, 'head'), axis=2)]
where the time goes in v1:
time: 164 us; the launch traced here: 163 us
  blocking collectives  108 us (66%)
  matrix products  32.3 us (20%)
  local copies, waits for them, and re-layouts  12.7 us (8%)
  other arithmetic  8.35 us (5%)
    psum x2, blocking collectives, body(): numerator, total = lax.psum((numerator, total), ('pts', 'head'))  81.5 us
    all_gather x1, blocking collectives, body(): full_fx = lax.all_gather(w_fx, 'head', axis=2, tiled=True)  11.1 us
    dot_general x2, matrix products, body(): jnp.dot(upper, w_down[layer_index], preferred_element_type=jnp.float32)  8.51 us
    all_gather x1, blocking collectives, body(): full_out = lax.all_gather(w_out, 'head', axis=1, tiled=True)  8.02 us
    all_gather x1, blocking collectives, body(): full_in = jnp.concatenate(lax.all_gather(w_in, 'head'), axis=2)  7.44 us
    dot_general x2, matrix products, body(): projected = jnp.dot(half_weights, wide, preferred_element_type=jnp.float32)  6.22 us
    sub x2, matrix products, body(): weights = jax.nn.softmax(logits, axis=-1) * live[:, None, None]  5.29 us
    dot_general x2, matrix products, body(): jnp.einsum('rs,rl->sl', half_weights, feats, preferred_element_type=jnp.f...  4.24 us

profile of v1, /device:TPU:0, one launch (start us, length us, event | category | flops | bytes accessed | tf_op | source)
XLA Modules:
  0.0 162.5 jit_solution(15274077115372126511)
XLA Ops:
  0.0 0.0 copy-start
  0.8 1.3 slice_bitcast_fusion.17
  2.2 1.3 slice_bitcast_fusion.16
  3.5 1.3 slice_bitcast_fusion.18
  4.7 1.3 slice_bitcast_fusion.14
  6.1 0.7 slice_bitcast_fusion.12
  6.8 0.1 copy.25
  6.9 0.1 copy.24
  7.0 11.1 %all_gather.14 = bf16[2,128,128]{1,2,0:T(8,128)(2,1)} all-gather(bf16[2,128,32]{1,2,0:T(8,128)(2,1)} %param.22), channel_id=1, replica_groups=mesh['pts'=8,'head'=4] {'head'}, dimensions={2}, use_global_device_ids=true | all-gather | bytes 81920 | tf_op jit(solution)/shard_map/all_gather | solution.py:57
  18.1 7.4 %all-gather = bf16[8,128,32]{1,2,0:T(8,128)(2,1)S(1)} all-gather(bf16[2,128,32]{1,2,0:T(8,128)(2,1)} %param.21), channel_id=2, replica_groups=mesh['pts'=8,'head'=4] {'head'}, dimensions={0}, use_global_device_ids=true | all-gather | bytes 81920 | tf_op jit(solution)/shard_map/all_gather | solution.py:56
  25.6 0.6 fusion.123
  26.2 8.0 %all_gather.15 = bf16[2,128,128]{2,1,0:T(8,128)(2,1)S(1)} all-gather(bf16[2,32,128]{2,1,0:T(8,128)(2,1)} %param.28), channel_id=1, replica_groups=mesh['pts'=8,'head'=4] {'head'}, dimensions={1}, use_global_device_ids=true | all-gather | bytes 81920 | tf_op jit(solution)/shard_map/all_gather | solution.py:58
  34.2 0.6 fusion.122
  34.8 0.2 broadcast_multiply_fusion
  35.0 0.7 mul.210
  35.7 0.7 mul.187
  36.4 0.0 copy-done
  36.5 0.2 copy.31
  36.7 0.0 copy-start.5
  36.7 0.0 copy-start.17
  36.8 0.1 convert_reduce_fusion
  36.9 0.2 fusion.33
  37.1 0.5 copy-done.5
  37.6 1.2 convolution_convert_fusion.1
  38.8 0.0 copy-done.11
  38.8 1.9 %fusion.124 = (f32[2304,4]{0,1:T(4,128)S(1)}, f32[2304,4,32]{0,2,1:T(8,128)}) fusion(bf16[4,32,128]{2,1,0:T(8,128)(2,1)S(1)} %bitcast.194, bf16[128,128]{0,1:T(8,128)(2,1)S(1)} %bitcast.198, f32[4]{0:T(128)S(1)} %copy-done.15, bf16[2304,128]{0,1:T(8,128)(2,1)S(1)} %copy.31, f32[128]{0:T(128)S(1)} %copy-done.17, f32[128]{0:T(128)S(1)} %copy-done.18, ...), kind=kOutput, calls=%fused_computation.173 | convolution fusion | flops 153944096 | bytes 1891344 | tf_op jit(solution)/shard_map/sub | solution.py:75
  40.7 2.1 %fusion.39 = f32[4,32,4,32]{3,1,2,0:T(8,128)S(1)} fusion(bf16[4,32,2304,1]{2,1,0,3:T(8,128)(2,1)} %bitcast.199, f32[2304]{0:T(1024)S(1)} %fusion.81, f32[2304,4,32]{0,2,1:T(8,128)} %get-tuple-element.38, f32[2304,4]{0,1:T(4,128)S(1)} %get-tuple-element.37), kind=kOutput, calls=%fused_computation.67 | convolution fusion | flops 76382208 | bytes 1881088 | tf_op jit(solution)/shard_map/rs,rl->sl/dot_general | solution.py:78
  42.8 0.0 copy-start.19
  42.8 0.0 copy-start.20
  42.8 0.0 copy-start.21
  42.9 0.2 fusion.57
  43.1 40.2 %all-reduce.1 = (f32[4,32,32]{2,1,0:T(8,128)S(1)}, f32[4,32]{1,0:T(4,128)S(1)}) all-reduce(f32[4,32,32]{2,1,0:T(8,128)S(1)} %pad_maximum_fusion, f32[4,32]{1,0:T(4,128)S(1)} %fusion.57), channel_id=1, replica_groups=mesh['pts'=8,'head'=4] {'pts','head'}, use_global_device_ids=true, to_apply=%region_4.5 | all-reduce | flops 4224 | bytes 33792 | tf_op jit(solution)/shard_map/psum | solution.py:81
  83.4 0.2 fusion.90
  83.6 0.2 fusion.88
  83.9 0.2 fusion.92
  84.1 0.2 fusion.127
  84.4 0.3 convolution_convert_fusion.7
  84.7 2.8 %fusion.128 = (f32[2304]{0:T(1024)S(1)}, f32[2304,128]{0,1:T(8,128)}) fusion(f32[128]{0:T(128)S(1)} %copy-done.14, bf16[4,32,32]{2,1,0:T(8,128)(2,1)S(1)} %convolution_convert_fusion.7, bf16[4,32,128]{2,1,0:T(8,128)(2,1)S(1)} %bitcast.197, f32[2304]{0:T(1024)S(1)} %fusion.81, f32[2304,4,32]{0,2,1:T(8,128)} %get-tuple-element.38, ...), kind=kOutput, calls=%fused_computation.175 | convolution fusion | flops 78624512 | bytes 3045888 | tf_op jit(solution)/shard_map/dot_general | solution.py:99
  87.5 1.4 multiply_reduce_fusion.2
  88.9 0.6 add_rsqrt_fusion.2
  89.5 4.5 %fusion.129 = (f32[2304]{0:T(1024)}, f32[2304,128]{0,1:T(8,128)S(1)}) fusion(f32[2304,128]{0,1:T(8,128)} %get-tuple-element.42, bf16[2,512,128]{2,1,0:T(8,128)(2,1)} %param.33, f32[128]{0:T(128)} %get-tuple-element.26, f32[128]{0:T(128)} %get-tuple-element.53, f32[2304]{0:T(1024)} %add_rsqrt_fusion.2, f32[2304]{0:T(1024)} %copy-done.7, ...), kind=kOutput, calls=%fused_computation.176 | convolution fusion | flops 617248512 | bytes 3835904 | tf_op jit(solution)/shard_map/dot_general | solution.py:108
  94.1 0.7 broadcast_multiply_fusion.3
  94.8 0.1 multiply_reduce_fusion.1
  94.9 0.0 copy-start.6
  95.0 0.4 add_convert_fusion.1
  95.4 0.8 copy-done.1
  96.2 1.1 convolution_convert_fusion
  97.3 3.4 %fusion.132 = (f32[2304,4]{0,1:T(4,128)}, f32[2304,4,32]{0,2,1:T(8,128)}) fusion(bf16[4,32,128]{2,1,0:T(8,128)(2,1)} %bitcast.193, bf16[2304,128]{0,1:T(8,128)(2,1)} %copy-done.1, bf16[128,128]{0,1:T(8,128)(2,1)} %bitcast.196, f32[4]{0:T(128)S(1)} %copy-done.13), kind=kOutput, calls=%fused_computation.177 | convolution fusion | flops 152174624 | bytes 1871888 | tf_op jit(solution)/shard_map/sub | solution.py:75
  100.8 2.1 %fusion.37 = f32[4,32,4,32]{3,1,2,0:T(8,128)S(1)} fusion(bf16[4,32,2304,1]{2,1,0,3:T(8,128)(2,1)} %bitcast.191, f32[2304]{0:T(1024)S(1)} %fusion.81, f32[2304,4,32]{0,2,1:T(8,128)} %get-tuple-element.46, f32[2304,4]{0,1:T(4,128)} %get-tuple-element.45), kind=kOutput, calls=%fused_computation.65 | convolution fusion | flops 76382208 | bytes 1881088 | tf_op jit(solution)/shard_map/rs,rl->sl/dot_general | solution.py:78
  102.9 0.6 pad_maximum_fusion.1
  103.5 0.2 fusion.59
  103.8 41.3 %all-reduce = (f32[4,32,32]{2,1,0:T(8,128)}, f32[4,32]{1,0:T(4,128)}) all-reduce(f32[4,32,32]{2,1,0:T(8,128)} %pad_maximum_fusion.1, f32[4,32]{1,0:T(4,128)S(1)} %fusion.59), channel_id=1, replica_groups=mesh['pts'=8,'head'=4] {'pts','head'}, use_global_device_ids=true, to_apply=%region_15.16 | all-reduce | flops 4224 | bytes 33792 | tf_op jit(solution)/shard_map/psum | solution.py:81
  145.1 0.7 broadcast_maximum_fusion
  145.7 1.1 fusion.84
  146.8 1.1 fusion.82
  147.9 1.1 fusion.86
  149.0 0.2 fusion.133
  149.3 0.9 convolution_convert_fusion.5
  150.2 3.4 %fusion.134 = (f32[2304]{0:T(1024)}, f32[2304,128]{0,1:T(8,128)}) fusion(f32[128]{0:T(128)} %get-tuple-element.27, f32[2304,128]{0,1:T(8,128)S(1)} %get-tuple-element.44, bf16[4,32,32]{2,1,0:T(8,128)(2,1)} %convolution_convert_fusion.5, bf16[4,32,128]{2,1,0:T(8,128)(2,1)} %bitcast.195, f32[2304]{0:T(1024)S(1)} %fusion.81, ...), kind=kOutput, calls=%fused_computation.179 | convolution fusion | flops 78329600 | bytes 3635712 | tf_op jit(solution)/shard_map/dot_general | solution.py:99
  153.6 0.8 broadcast_multiply_fusion.2
  154.4 1.4 multiply_reduce_fusion
  155.8 0.6 add_rsqrt_fusion
  156.5 4.0 %fusion.27 = bf16[2304,128]{0,1:T(8,128)(2,1)} fusion(f32[2304,128]{0,1:T(8,128)S(1)} %copy-done.4, f32[128]{0:T(128)S(1)} %copy-done.16, f32[128]{0:T(128)} %get-tuple-element.54, f32[2304]{0:T(1024)} %add_rsqrt_fusion, f32[2304]{0:T(1024)S(1)} %broadcast_multiply_fusion.2, bf16[2,512,128]{2,1,0:T(8,128)(2,1)} %param.33, bf16[2,128,512]{2,1,0:T(8,128)(2,1)} %param.32), kind=kOutput, calls=%fused_computation.35 | convolution fusion | flops 616660992 | bytes 3236864 | tf_op jit(solution)/shard_map/dot_general | solution.py:108
  160.4 2.1 %copy.27 = bf16[2304,128]{1,0:T(8,128)(2,1)} copy(bf16[2304,128]{0,1:T(8,128)(2,1)} %fusion.27) | data formatting | bytes 1179648 | tf_op jit(solution)/shard_map/convert_element_type | solution.py:109
  (46 shorter events, 0.2 us)
Async XLA Ops:
  0.0 36.4 %copy-start = (bf16[9216,128]{1,0:T(8,128)(2,1)S(1)}, bf16[9216,128]{1,0:T(8,128)(2,1)}, u32[]{:S(2)}) copy-start(bf16[9216,128]{1,0:T(8,128)(2,1)} %param.17) | copy-start | bytes 7077892
  36.7 0.8 copy-start.5
  36.7 0.8 copy-start.17
  36.8 0.8 copy-start.18
  36.9 2.0 %copy-start.9 = (bf16[128,128]{0,1:T(8,128)(2,1)S(1)}, bf16[128,128]{0,1:T(8,128)(2,1)}, u32[]{:S(2)}) copy-start(bf16[128,128]{0,1:T(8,128)(2,1)} %mul.187) | copy-start | bytes 98308
  36.9 1.9 %copy-start.11 = (bf16[1,128,4,32]{1,3,0,2:T(8,128)(2,1)S(1)}, bf16[1,128,4,32]{1,3,0,2:T(8,128)(2,1)}, u32[]{:S(2)}) copy-start(bf16[1,128,4,32]{1,3,0,2:T(8,128)(2,1)} %get-tuple-element.20) | copy-start | bytes 98308
  36.9 1.9 %copy-start.15 = (f32[4]{0:T(128)S(1)}, f32[4]{0:T(128)}, u32[]{:S(2)}) copy-start(f32[4]{0:T(128)} %get-tuple-element.30) | copy-start | bytes 52
  40.7 2.2 %copy-start.2 = (f32[2304,4,32]{0,2,1:T(8,128)S(1)}, f32[2304,4,32]{0,2,1:T(8,128)}, u32[]{:S(2)}) copy-start(f32[2304,4,32]{0,2,1:T(8,128)} %get-tuple-element.38) | copy-start | bytes 3538948
  42.8 40.5 %copy-start.19 = (bf16[2,32,32]{2,1,0:T(8,128)(2,1)S(1)}, bf16[2,32,32]{2,1,0:T(8,128)(2,1)}, u32[]{:S(2)}) copy-start(bf16[2,32,32]{2,1,0:T(8,128)(2,1)} %param.26) | copy-start | bytes 12292
  42.8 40.8 %copy-start.20 = (bf16[2,32,32]{2,1,0:T(8,128)(2,1)S(1)}, bf16[2,32,32]{2,1,0:T(8,128)(2,1)}, u32[]{:S(2)}) copy-start(bf16[2,32,32]{2,1,0:T(8,128)(2,1)} %param.27) | copy-start | bytes 12292
  42.8 41.0 %copy-start.21 = (bf16[2,32,32]{2,1,0:T(8,128)(2,1)S(1)}, bf16[2,32,32]{2,1,0:T(8,128)(2,1)}, u32[]{:S(2)}) copy-start(bf16[2,32,32]{2,1,0:T(8,128)(2,1)} %param.25) | copy-start | bytes 12292
  42.9 41.8 %copy-start.10 = (bf16[1,128,128]{2,1,0:T(8,128)(2,1)S(1)}, bf16[1,128,128]{2,1,0:T(8,128)(2,1)}, u32[]{:S(2)}) copy-start(bf16[1,128,128]{2,1,0:T(8,128)(2,1)} %get-tuple-element.18) | copy-start | bytes 98308
  42.9 41.8 %copy-start.14 = (f32[128]{0:T(128)S(1)}, f32[128]{0:T(128)}, u32[]{:S(2)}) copy-start(f32[128]{0:T(128)} %get-tuple-element.28) | copy-start | bytes 1540
  87.5 1.4 copy-start.7
  94.1 0.9 copy-start.12
  94.9 1.3 copy-start.6
  95.3 0.8 copy-start.1
  96.2 1.1 copy-start.13
  100.7 2.8 %copy-start.3 = (f32[2304,4,32]{0,2,1:T(8,128)S(1)}, f32[2304,4,32]{0,2,1:T(8,128)}, u32[]{:S(2)}) copy-start(f32[2304,4,32]{0,2,1:T(8,128)} %get-tuple-element.46) | copy-start | bytes 3538948
  100.7 2.8 %copy-start.8 = (f32[2304,4]{0,1:T(4,128)S(1)}, f32[2304,4]{0,1:T(4,128)}, u32[]{:S(2)}) copy-start(f32[2304,4]{0,1:T(4,128)} %get-tuple-element.45) | copy-start | bytes 110596
  153.6 2.8 %copy-start.4 = (f32[2304,128]{0,1:T(8,128)S(1)}, f32[2304,128]{0,1:T(8,128)}, u32[]{:S(2)}) copy-start(f32[2304,128]{0,1:T(8,128)} %get-tuple-element.50) | copy-start | bytes 3538948
  153.6 2.8 %copy-start.16 = (f32[128]{0:T(128)S(1)}, f32[128]{0:T(128)}, u32[]{:S(2)}) copy-start(f32[128]{0:T(128)} %get-tuple-element.25) | copy-start | bytes 1540
